TPU v7x, 32 devices: a whole 2x2x4 slice. The times are simulated.
32 devices in a mesh: orb: 4 (over x, core), gx: 2 (over y), gyz: 4 (over z).
Axes of the slice: x: 2, y: 2, z: 4, core: 2. Of those that a mesh axis runs over, the one named last changes fastest.
Arguments:
- orbitals: float32 [2, 12, 32, 32, 128], P(None, 'orb', 'gx', 'gyz'), parts along dimension 1, may hold values from -12 to 12
- potential: float32 [32, 32, 128], P('gx', 'gyz'), may hold values from -8 to 60
Outputs:
- evolved: float32 [2, 12, 32, 32, 128], P(None, 'orb', 'gx', 'gyz'), parts along dimension 1
- residual: float32 [2, 12, 32, 32, 128], P(None, 'orb', 'gx', 'gyz'), parts along dimension 1
There are 4 independent parts, one for each index of `orb`. A program takes and returns all parts, laid end to end along the dimension named above; an argument that names none is the same for every part. Nothing has to cross between parts.
All inputs are finite; a program needn't handle non-finite values.
Results may differ from a plain program's by a relative error of at most 0.0003.
Values sent between devices are 32-bit elements; how exact they have to be, the bound alone decides.
A program may use at most 64 MiB of HBM per device.

v0:
```python
import jax
import jax.numpy as jnp
from jax import lax
from jax.sharding import PartitionSpec as P

ITERS = 4


SPACING = 0.25
HALF_STEP = 0.05
COEFF_NEAR = 4.0 / 3.0
COEFF_FAR = -1.0 / 12.0
COEFF_SELF = -2.5


def with_halo(array, sides, width):
    for axis, dim in sides:
        size, length = (lax.axis_size(axis), array.shape[dim])
        up = [(i, (i + 1) % size) for i in range(size - 1)]
        down = [(j, i) for i, j in up]
        last = lax.slice_in_dim(array, length - width, length, axis=dim)
        leading = lax.slice_in_dim(array, 0, width, axis=dim)
        before = lax.ppermute(last, axis, up)
        after = lax.ppermute(leading, axis, down)
        array = jnp.concatenate([before, array, after], axis=dim)
    return array


def laplace_apply(padded, potential):
    extent = (padded.shape[2] - 4, padded.shape[3] - 4, padded.shape[4] - 4)

    def window(shift_x, shift_y, shift_z):
        return padded[
            :,
            :,
            2 + shift_x : 2 + shift_x + extent[0],
            2 + shift_y : 2 + shift_y + extent[1],
            2 + shift_z : 2 + shift_z + extent[2],
        ]

    center = window(0, 0, 0)
    summed = 3.0 * COEFF_SELF * center
    for offset, weight in ((1, COEFF_NEAR), (2, COEFF_FAR)):
        summed = summed + weight * (
            window(offset, 0, 0)
            + window(-offset, 0, 0)
            + window(0, offset, 0)
            + window(0, -offset, 0)
            + window(0, 0, offset)
            + window(0, 0, -offset)
        )
    return -0.5 / SPACING**2 * summed + potential * center


def pad_depth(vector):
    return jnp.pad(vector, ((0, 0), (0, 0), (0, 0), (0, 0), (2, 2)))


def system(vector, applied):
    return jnp.stack([vector[0] - HALF_STEP * applied[1], vector[1] + HALF_STEP * applied[0]])


def precondition(vector, potential):
    diagonal = HALF_STEP * (3.75 / SPACING**2 + potential)
    divisor = 1.0 + diagonal * diagonal
    return jnp.stack(
        [(vector[0] + diagonal * vector[1]) / divisor, (vector[1] - diagonal * vector[0]) / divisor]
    )


def braket(left, right):
    real_part = jnp.sum(left[0] * right[0] + left[1] * right[1], axis=(1, 2, 3))
    imag_part = jnp.sum(left[0] * right[1] - left[1] * right[0], axis=(1, 2, 3))
    return (real_part, imag_part)


def times_complex(first, second):
    return (
        first[0] * second[0] - first[1] * second[1],
        first[0] * second[1] + first[1] * second[0],
    )


def divide_complex(first, second):
    modulus = second[0] * second[0] + second[1] * second[1]
    return (
        (first[0] * second[0] + first[1] * second[1]) / modulus,
        (first[1] * second[0] - first[0] * second[1]) / modulus,
    )


def scale_complex(coeff, vector):
    real_coef = coeff[0][:, None, None, None]
    imag_coef = coeff[1][:, None, None, None]
    return jnp.stack(
        [
            real_coef * vector[0] - imag_coef * vector[1],
            real_coef * vector[1] + imag_coef * vector[0],
        ]
    )


def shards(orbitals, potential):

    def apply_shallow(vector):
        padded = with_halo(vector, (("gx", 2), ("gyz", 3)), 2)
        return laplace_apply(pad_depth(padded), potential)

    h_orbitals = apply_shallow(orbitals)
    residual = jnp.stack([2.0 * HALF_STEP * h_orbitals[1], -2.0 * HALF_STEP * h_orbitals[0]])
    evolved = orbitals
    shadow = residual
    direction = residual
    rho_now = lax.psum(braket(shadow, residual), ("gx", "gyz"))
    for iteration in range(ITERS):
        dir_hat = precondition(direction, potential)
        image = system(dir_hat, apply_shallow(dir_hat))
        alpha_step = divide_complex(rho_now, lax.psum(braket(shadow, image), ("gx", "gyz")))
        half_step = residual - scale_complex(alpha_step, image)
        half_hat = precondition(half_step, potential)
        second = system(half_hat, apply_shallow(half_hat))
        cross_local = braket(second, half_step)
        norm_local = jnp.sum(second * second, axis=(0, 2, 3, 4))
        shadow_half = braket(shadow, half_step)
        shadow_second = braket(shadow, second)
        summed = lax.psum(
            (
                cross_local[0],
                cross_local[1],
                norm_local,
                shadow_half[0],
                shadow_half[1],
                shadow_second[0],
                shadow_second[1],
            ),
            ("gx", "gyz"),
        )
        cross_real, cross_imag, norm_second = (summed[0], summed[1], summed[2])
        omega_step = (cross_real / norm_second, cross_imag / norm_second)
        evolved = evolved + scale_complex(alpha_step, dir_hat) + scale_complex(omega_step, half_hat)
        residual = half_step - scale_complex(omega_step, second)
        if iteration + 1 < ITERS:
            along_second = times_complex(omega_step, (summed[5], summed[6]))
            rho_next = (summed[3] - along_second[0], summed[4] - along_second[1])
            beta_step = times_complex(
                divide_complex(rho_next, rho_now), divide_complex(alpha_step, omega_step)
            )
            direction = residual + scale_complex(
                beta_step, direction - scale_complex(omega_step, image)
            )
            rho_now = rho_next
    return (evolved, residual)


def solution(mesh):
    return jax.shard_map(
        shards,
        mesh=mesh,
        in_specs=(P(None, "orb", "gx", "gyz", None), P("gx", "gyz", None)),
        out_specs=(P(None, "orb", "gx", "gyz", None), P(None, "orb", "gx", "gyz", None)),
        check_vma=False,
    )
```

profile of v0, /device:TPU:28, one launch (start us, length us, event | category | flops | bytes accessed | tf_op | source)
XLA Modules:
  0.0 350.5 jit_solution(2603612143626635180)
XLA Ops:
  2.8 4.5 %collective-permute-start = (f32[2,3,2,8,128]{4,3,2,1,0:T(8,128)S(1)}, f32[2,3,2,8,128]{4,3,2,1,0:T(8,128)S(1)}, u32[]{:S(2)}, u32[]{:S(2)}) collective-permute-start(f32[2,3,2,8,128]{4,3,2,1,0:T(8,128)S(1)} %get-tuple-element.243), channel_id=1, source_target_pairs={{4,0},{5,1},{6,2},{7,3},{12,8},{13,9},{14,10},{15,11},{20,16},{21,... | collective-permute-start | bytes 147464 | tf_op jit(solution)/shard_map/ppermute | solution.py:24
  10.5 4.6 %collective-permute-start.2 = (f32[2,3,20,2,128]{4,3,2,1,0:T(2,128)S(1)}, f32[2,3,20,2,128]{4,3,2,1,0:T(2,128)S(1)}, u32[]{:S(2)}, u32[]{:S(2)}) collective-permute-start(f32[2,3,20,2,128]{4,3,2,1,0:T(2,128)S(1)} %get-tuple-element.159), channel_id=1, source_target_pairs={{1,0},{2,1},{3,2},{5,4},{6,5},{7,6},{9,8},{10,9},{11,10},{13,12},{... | collective-permute-start | bytes 368648 | tf_op jit(solution)/shard_map/ppermute | solution.py:24
  20.6 4.5 %collective-permute-start.4 = (f32[2,3,2,8,128]{4,3,2,1,0:T(8,128)S(1)}, f32[2,3,2,8,128]{4,3,2,1,0:T(8,128)S(1)}, u32[]{:S(2)}, u32[]{:S(2)}) collective-permute-start(f32[2,3,2,8,128]{4,3,2,1,0:T(8,128)S(1)} %get-tuple-element.239), channel_id=1, source_target_pairs={{4,0},{5,1},{6,2},{7,3},{12,8},{13,9},{14,10},{15,11},{20,16},{21,... | collective-permute-start | bytes 147464 | tf_op jit(solution)/shard_map/ppermute | solution.py:24
  28.2 5.0 %collective-permute-start.6 = (f32[2,3,20,2,128]{4,3,2,1,0:T(2,128)S(1)}, f32[2,3,20,2,128]{4,3,2,1,0:T(2,128)S(1)}, u32[]{:S(2)}, u32[]{:S(2)}) collective-permute-start(f32[2,3,20,2,128]{4,3,2,1,0:T(2,128)S(1)} %get-tuple-element.157), channel_id=1, source_target_pairs={{1,0},{2,1},{3,2},{5,4},{6,5},{7,6},{9,8},{10,9},{11,10},{13,12},{... | collective-permute-start | bytes 368648 | tf_op jit(solution)/shard_map/ppermute | solution.py:24
  37.7 20.0 %all-reduce.16 = (f32[3]{0:T(128)S(1)}, f32[3]{0:T(128)S(1)}, f32[3]{0:T(128)S(1)}, f32[3]{0:T(128)S(1)}) all-reduce(f32[3]{0:T(128)S(1)} %get-tuple-element.43, f32[3]{0:T(128)S(1)} %get-tuple-element.3, f32[3]{0:T(128)S(1)} %get-tuple-element.42, f32[3]{0:T(128)S(1)} %get-tuple-element.2), channel_id=1, replica_groups=mesh['orb'=4,'gx'=2,'gyz'=4] {'gx','gyz'}, use_global_device_ids=true, to_apply=%region_1.2 | all-reduce | flops 12 | bytes 96 | tf_op jit(solution)/shard_map/psum | solution.py:114
  60.2 4.5 %collective-permute-start.8 = (f32[2,3,2,8,128]{4,3,2,1,0:T(8,128)S(1)}, f32[2,3,2,8,128]{4,3,2,1,0:T(8,128)S(1)}, u32[]{:S(2)}, u32[]{:S(2)}) collective-permute-start(f32[2,3,2,8,128]{4,3,2,1,0:T(8,128)S(1)} %get-tuple-element.233), channel_id=1, source_target_pairs={{4,0},{5,1},{6,2},{7,3},{12,8},{13,9},{14,10},{15,11},{20,16},{21,... | collective-permute-start | bytes 147464 | tf_op jit(solution)/shard_map/ppermute | solution.py:24
  67.8 4.6 %collective-permute-start.10 = (f32[2,3,20,2,128]{4,3,2,1,0:T(2,128)S(1)}, f32[2,3,20,2,128]{4,3,2,1,0:T(2,128)S(1)}, u32[]{:S(2)}, u32[]{:S(2)}) collective-permute-start(f32[2,3,20,2,128]{4,3,2,1,0:T(2,128)S(1)} %get-tuple-element.155), channel_id=1, source_target_pairs={{1,0},{2,1},{3,2},{5,4},{6,5},{7,6},{9,8},{10,9},{11,10},{13,12},{... | collective-permute-start | bytes 368648 | tf_op jit(solution)/shard_map/ppermute | solution.py:24
  77.2 19.6 %all-reduce.15 = (f32[3]{0:T(128)S(1)}, f32[3]{0:T(128)S(1)}, f32[3]{0:T(128)S(1)}, f32[3]{0:T(128)S(1)}, f32[3]{0:T(128)S(1)}, /*index=5*/f32[3]{0:T(128)S(1)}, f32[3]{0:T(128)S(1)}) all-reduce(f32[3]{0:T(128)S(1)} %get-tuple-element.40, f32[3]{0:T(128)S(1)} %fusion.80, ...), channel_id=1, replica_groups=mesh['orb'=4,'gx'=2,'gyz'=4] {'gx','gyz'}, use_global_device_ids=true, to_apply=%region_13.14 | all-reduce | flops 21 | bytes 168 | tf_op jit(solution)/shard_map/psum | solution.py:126
  100.2 4.5 %collective-permute-start.12 = (f32[2,3,2,8,128]{4,3,2,1,0:T(8,128)S(1)}, f32[2,3,2,8,128]{4,3,2,1,0:T(8,128)S(1)}, u32[]{:S(2)}, u32[]{:S(2)}) collective-permute-start(f32[2,3,2,8,128]{4,3,2,1,0:T(8,128)S(1)} %get-tuple-element.227), channel_id=1, source_target_pairs={{4,0},{5,1},{6,2},{7,3},{12,8},{13,9},{14,10},{15,11},{20,16},{21,... | collective-permute-start | bytes 147464 | tf_op jit(solution)/shard_map/ppermute | solution.py:24
  107.8 4.6 %collective-permute-start.14 = (f32[2,3,20,2,128]{4,3,2,1,0:T(2,128)S(1)}, f32[2,3,20,2,128]{4,3,2,1,0:T(2,128)S(1)}, u32[]{:S(2)}, u32[]{:S(2)}) collective-permute-start(f32[2,3,20,2,128]{4,3,2,1,0:T(2,128)S(1)} %get-tuple-element.153), channel_id=1, source_target_pairs={{1,0},{2,1},{3,2},{5,4},{6,5},{7,6},{9,8},{10,9},{11,10},{13,12},{... | collective-permute-start | bytes 368648 | tf_op jit(solution)/shard_map/ppermute | solution.py:24
  116.8 19.7 %all-reduce.14 = (f32[3]{0:T(128)S(1)}, f32[3]{0:T(128)S(1)}) all-reduce(f32[3]{0:T(128)S(1)} %get-tuple-element.23, f32[3]{0:T(128)S(1)} %get-tuple-element.22), channel_id=1, replica_groups=mesh['orb'=4,'gx'=2,'gyz'=4] {'gx','gyz'}, use_global_device_ids=true, to_apply=%region_25.26 | all-reduce | flops 6 | bytes 48 | tf_op jit(solution)/shard_map/psum | solution.py:118
  139.6 4.5 %collective-permute-start.16 = (f32[2,3,2,8,128]{4,3,2,1,0:T(8,128)S(1)}, f32[2,3,2,8,128]{4,3,2,1,0:T(8,128)S(1)}, u32[]{:S(2)}, u32[]{:S(2)}) collective-permute-start(f32[2,3,2,8,128]{4,3,2,1,0:T(8,128)S(1)} %get-tuple-element.223), channel_id=1, source_target_pairs={{4,0},{5,1},{6,2},{7,3},{12,8},{13,9},{14,10},{15,11},{20,16},{21,... | collective-permute-start | bytes 147464 | tf_op jit(solution)/shard_map/ppermute | solution.py:24
  147.3 4.7 %collective-permute-start.18 = (f32[2,3,20,2,128]{4,3,2,1,0:T(2,128)S(1)}, f32[2,3,20,2,128]{4,3,2,1,0:T(2,128)S(1)}, u32[]{:S(2)}, u32[]{:S(2)}) collective-permute-start(f32[2,3,20,2,128]{4,3,2,1,0:T(2,128)S(1)} %get-tuple-element.151), channel_id=1, source_target_pairs={{1,0},{2,1},{3,2},{5,4},{6,5},{7,6},{9,8},{10,9},{11,10},{13,12},{... | collective-permute-start | bytes 368648 | tf_op jit(solution)/shard_map/ppermute | solution.py:24
  157.2 19.8 %all-reduce.13 = (f32[3]{0:T(128)S(1)}, f32[3]{0:T(128)S(1)}, f32[3]{0:T(128)S(1)}, f32[3]{0:T(128)S(1)}, f32[3]{0:T(128)S(1)}, /*index=5*/f32[3]{0:T(128)S(1)}, f32[3]{0:T(128)S(1)}) all-reduce(f32[3]{0:T(128)} %get-tuple-element.36, f32[3]{0:T(128)S(1)} %fusion.81, ...), channel_id=1, replica_groups=mesh['orb'=4,'gx'=2,'gyz'=4] {'gx','gyz'}, use_global_device_ids=true, to_apply=%region_31.32 | all-reduce | flops 21 | bytes 168 | tf_op jit(solution)/shard_map/psum | solution.py:126
  182.9 4.5 %collective-permute-start.20 = (f32[2,3,2,8,128]{4,3,2,1,0:T(8,128)S(1)}, f32[2,3,2,8,128]{4,3,2,1,0:T(8,128)S(1)}, u32[]{:S(2)}, u32[]{:S(2)}) collective-permute-start(f32[2,3,2,8,128]{4,3,2,1,0:T(8,128)S(1)} %get-tuple-element.217), channel_id=1, source_target_pairs={{4,0},{5,1},{6,2},{7,3},{12,8},{13,9},{14,10},{15,11},{20,16},{21,... | collective-permute-start | bytes 147464 | tf_op jit(solution)/shard_map/ppermute | solution.py:24
  190.6 4.6 %collective-permute-start.22 = (f32[2,3,20,2,128]{4,3,2,1,0:T(2,128)S(1)}, f32[2,3,20,2,128]{4,3,2,1,0:T(2,128)S(1)}, u32[]{:S(2)}, u32[]{:S(2)}) collective-permute-start(f32[2,3,20,2,128]{4,3,2,1,0:T(2,128)S(1)} %get-tuple-element.149), channel_id=1, source_target_pairs={{1,0},{2,1},{3,2},{5,4},{6,5},{7,6},{9,8},{10,9},{11,10},{13,12},{... | collective-permute-start | bytes 368648 | tf_op jit(solution)/shard_map/ppermute | solution.py:24
  199.6 19.5 %all-reduce.12 = (f32[3]{0:T(128)S(1)}, f32[3]{0:T(128)S(1)}) all-reduce(f32[3]{0:T(128)S(1)} %get-tuple-element.15, f32[3]{0:T(128)S(1)} %get-tuple-element.14), channel_id=1, replica_groups=mesh['orb'=4,'gx'=2,'gyz'=4] {'gx','gyz'}, use_global_device_ids=true, to_apply=%region_43.44 | all-reduce | flops 6 | bytes 48 | tf_op jit(solution)/shard_map/psum | solution.py:118
  222.2 4.5 %collective-permute-start.24 = (f32[2,3,2,8,128]{4,3,2,1,0:T(8,128)S(1)}, f32[2,3,2,8,128]{4,3,2,1,0:T(8,128)S(1)}, u32[]{:S(2)}, u32[]{:S(2)}) collective-permute-start(f32[2,3,2,8,128]{4,3,2,1,0:T(8,128)S(1)} %get-tuple-element.213), channel_id=1, source_target_pairs={{4,0},{5,1},{6,2},{7,3},{12,8},{13,9},{14,10},{15,11},{20,16},{21,... | collective-permute-start | bytes 147464 | tf_op jit(solution)/shard_map/ppermute | solution.py:24
  229.9 4.6 %collective-permute-start.26 = (f32[2,3,20,2,128]{4,3,2,1,0:T(2,128)S(1)}, f32[2,3,20,2,128]{4,3,2,1,0:T(2,128)S(1)}, u32[]{:S(2)}, u32[]{:S(2)}) collective-permute-start(f32[2,3,20,2,128]{4,3,2,1,0:T(2,128)S(1)} %get-tuple-element.147), channel_id=1, source_target_pairs={{1,0},{2,1},{3,2},{5,4},{6,5},{7,6},{9,8},{10,9},{11,10},{13,12},{... | collective-permute-start | bytes 368648 | tf_op jit(solution)/shard_map/ppermute | solution.py:24
  240.4 20.6 %all-reduce.11 = (f32[3]{0:T(128)}, f32[3]{0:T(128)}, f32[3]{0:T(128)}, f32[3]{0:T(128)}, f32[3]{0:T(128)}, /*index=5*/f32[3]{0:T(128)}, f32[3]{0:T(128)}) all-reduce(f32[3]{0:T(128)} %get-tuple-element.32, f32[3]{0:T(128)} %fusion.82, f32[3]{0:T(128)} %get-tuple-element.33, ...), channel_id=1, replica_groups=mesh['orb'=4,'gx'=2,'gyz'=4] {'gx','gyz'}, use_global_device_ids=true, to_apply=%region_49.50 | all-reduce | flops 21 | bytes 168 | tf_op jit(solution)/shard_map/psum | solution.py:126
  274.4 4.6 %collective-permute-start.30 = (f32[2,3,20,2,128]{4,3,2,1,0:T(2,128)S(1)}, f32[2,3,20,2,128]{4,3,2,1,0:T(2,128)S(1)}, u32[]{:S(2)}, u32[]{:S(2)}) collective-permute-start(f32[2,3,20,2,128]{4,3,2,1,0:T(2,128)S(1)} %get-tuple-element.145), channel_id=1, source_target_pairs={{1,0},{2,1},{3,2},{5,4},{6,5},{7,6},{9,8},{10,9},{11,10},{13,12},{... | collective-permute-start | bytes 368648 | tf_op jit(solution)/shard_map/ppermute | solution.py:24
  283.9 19.9 %all-reduce.10 = (f32[3]{0:T(128)S(1)}, f32[3]{0:T(128)S(1)}) all-reduce(f32[3]{0:T(128)S(1)} %get-tuple-element.7, f32[3]{0:T(128)S(1)} %get-tuple-element.6), channel_id=1, replica_groups=mesh['orb'=4,'gx'=2,'gyz'=4] {'gx','gyz'}, use_global_device_ids=true, to_apply=%region_61.62 | all-reduce | flops 6 | bytes 48 | tf_op jit(solution)/shard_map/psum | solution.py:118
  316.6 4.6 %collective-permute-start.34 = (f32[2,3,20,2,128]{4,3,2,1,0:T(2,128)S(1)}, f32[2,3,20,2,128]{4,3,2,1,0:T(2,128)S(1)}, u32[]{:S(2)}, u32[]{:S(2)}) collective-permute-start(f32[2,3,20,2,128]{4,3,2,1,0:T(2,128)S(1)} %get-tuple-element.143), channel_id=1, source_target_pairs={{1,0},{2,1},{3,2},{5,4},{6,5},{7,6},{9,8},{10,9},{11,10},{13,12},{... | collective-permute-start | bytes 368648 | tf_op jit(solution)/shard_map/ppermute | solution.py:24
  326.4 19.6 %all-reduce.9 = (f32[3]{0:T(128)S(1)}, f32[3]{0:T(128)S(1)}, f32[3]{0:T(128)S(1)}) all-reduce(f32[3]{0:T(128)S(1)} %get-tuple-element.5, f32[3]{0:T(128)S(1)} %fusion.83, f32[3]{0:T(128)S(1)} %get-tuple-element.4), channel_id=1, replica_groups=mesh['orb'=4,'gx'=2,'gyz'=4] {'gx','gyz'}, use_global_device_ids=true, to_apply=%region_67.68 | all-reduce | flops 9 | bytes 72 | tf_op jit(solution)/shard_map/psum | solution.py:126
  (247 shorter events, 116.6 us)
Async XLA Ops:
  2.8 6.3 %collective-permute-start = (f32[2,3,2,8,128]{4,3,2,1,0:T(8,128)S(1)}, f32[2,3,2,8,128]{4,3,2,1,0:T(8,128)S(1)}, u32[]{:S(2)}, u32[]{:S(2)}) collective-permute-start(f32[2,3,2,8,128]{4,3,2,1,0:T(8,128)S(1)} %get-tuple-element.243), channel_id=1, source_target_pairs={{4,0},{5,1},{6,2},{7,3},{12,8},{13,9},{14,10},{15,11},{20,16},{21,... | collective-permute-start | bytes 147464 | tf_op jit(solution)/shard_map/ppermute | solution.py:24
  9.2 6.8 %collective-permute-start.3 = (f32[2,3,20,2,128]{4,3,2,1,0:T(2,128)S(1)}, f32[2,3,20,2,128]{4,3,2,1,0:T(2,128)S(1)}, u32[]{:S(2)}, u32[]{:S(2)}) collective-permute-start(f32[2,3,20,2,128]{4,3,2,1,0:T(2,128)S(1)} %get-tuple-element.158), channel_id=1, source_target_pairs={{0,1},{1,2},{2,3},{4,5},{5,6},{6,7},{8,9},{9,10},{10,11},{12,13},{... | collective-permute-start | bytes 368648 | tf_op jit(solution)/shard_map/ppermute | solution.py:23
  10.5 7.0 %collective-permute-start.2 = (f32[2,3,20,2,128]{4,3,2,1,0:T(2,128)S(1)}, f32[2,3,20,2,128]{4,3,2,1,0:T(2,128)S(1)}, u32[]{:S(2)}, u32[]{:S(2)}) collective-permute-start(f32[2,3,20,2,128]{4,3,2,1,0:T(2,128)S(1)} %get-tuple-element.159), channel_id=1, source_target_pairs={{1,0},{2,1},{3,2},{5,4},{6,5},{7,6},{9,8},{10,9},{11,10},{13,12},{... | collective-permute-start | bytes 368648 | tf_op jit(solution)/shard_map/ppermute | solution.py:24
  20.6 6.3 %collective-permute-start.4 = (f32[2,3,2,8,128]{4,3,2,1,0:T(8,128)S(1)}, f32[2,3,2,8,128]{4,3,2,1,0:T(8,128)S(1)}, u32[]{:S(2)}, u32[]{:S(2)}) collective-permute-start(f32[2,3,2,8,128]{4,3,2,1,0:T(8,128)S(1)} %get-tuple-element.239), channel_id=1, source_target_pairs={{4,0},{5,1},{6,2},{7,3},{12,8},{13,9},{14,10},{15,11},{20,16},{21,... | collective-permute-start | bytes 147464 | tf_op jit(solution)/shard_map/ppermute | solution.py:24
  26.9 7.2 %collective-permute-start.7 = (f32[2,3,20,2,128]{4,3,2,1,0:T(2,128)S(1)}, f32[2,3,20,2,128]{4,3,2,1,0:T(2,128)S(1)}, u32[]{:S(2)}, u32[]{:S(2)}) collective-permute-start(f32[2,3,20,2,128]{4,3,2,1,0:T(2,128)S(1)} %get-tuple-element.156), channel_id=1, source_target_pairs={{0,1},{1,2},{2,3},{4,5},{5,6},{6,7},{8,9},{9,10},{10,11},{12,13},{... | collective-permute-start | bytes 368648 | tf_op jit(solution)/shard_map/ppermute | solution.py:23
  28.2 7.4 %collective-permute-start.6 = (f32[2,3,20,2,128]{4,3,2,1,0:T(2,128)S(1)}, f32[2,3,20,2,128]{4,3,2,1,0:T(2,128)S(1)}, u32[]{:S(2)}, u32[]{:S(2)}) collective-permute-start(f32[2,3,20,2,128]{4,3,2,1,0:T(2,128)S(1)} %get-tuple-element.157), channel_id=1, source_target_pairs={{1,0},{2,1},{3,2},{5,4},{6,5},{7,6},{9,8},{10,9},{11,10},{13,12},{... | collective-permute-start | bytes 368648 | tf_op jit(solution)/shard_map/ppermute | solution.py:24
  66.5 6.8 %collective-permute-start.11 = (f32[2,3,20,2,128]{4,3,2,1,0:T(2,128)S(1)}, f32[2,3,20,2,128]{4,3,2,1,0:T(2,128)S(1)}, u32[]{:S(2)}, u32[]{:S(2)}) collective-permute-start(f32[2,3,20,2,128]{4,3,2,1,0:T(2,128)S(1)} %get-tuple-element.154), channel_id=1, source_target_pairs={{0,1},{1,2},{2,3},{4,5},{5,6},{6,7},{8,9},{9,10},{10,11},{12,13},{... | collective-permute-start | bytes 368648 | tf_op jit(solution)/shard_map/ppermute | solution.py:23
  67.8 7.0 %collective-permute-start.10 = (f32[2,3,20,2,128]{4,3,2,1,0:T(2,128)S(1)}, f32[2,3,20,2,128]{4,3,2,1,0:T(2,128)S(1)}, u32[]{:S(2)}, u32[]{:S(2)}) collective-permute-start(f32[2,3,20,2,128]{4,3,2,1,0:T(2,128)S(1)} %get-tuple-element.155), channel_id=1, source_target_pairs={{1,0},{2,1},{3,2},{5,4},{6,5},{7,6},{9,8},{10,9},{11,10},{13,12},{... | collective-permute-start | bytes 368648 | tf_op jit(solution)/shard_map/ppermute | solution.py:24
  100.2 6.3 %collective-permute-start.12 = (f32[2,3,2,8,128]{4,3,2,1,0:T(8,128)S(1)}, f32[2,3,2,8,128]{4,3,2,1,0:T(8,128)S(1)}, u32[]{:S(2)}, u32[]{:S(2)}) collective-permute-start(f32[2,3,2,8,128]{4,3,2,1,0:T(8,128)S(1)} %get-tuple-element.227), channel_id=1, source_target_pairs={{4,0},{5,1},{6,2},{7,3},{12,8},{13,9},{14,10},{15,11},{20,16},{21,... | collective-permute-start | bytes 147464 | tf_op jit(solution)/shard_map/ppermute | solution.py:24
  106.5 6.8 %collective-permute-start.15 = (f32[2,3,20,2,128]{4,3,2,1,0:T(2,128)S(1)}, f32[2,3,20,2,128]{4,3,2,1,0:T(2,128)S(1)}, u32[]{:S(2)}, u32[]{:S(2)}) collective-permute-start(f32[2,3,20,2,128]{4,3,2,1,0:T(2,128)S(1)} %get-tuple-element.152), channel_id=1, source_target_pairs={{0,1},{1,2},{2,3},{4,5},{5,6},{6,7},{8,9},{9,10},{10,11},{12,13},{... | collective-permute-start | bytes 368648 | tf_op jit(solution)/shard_map/ppermute | solution.py:23
  107.8 7.0 %collective-permute-start.14 = (f32[2,3,20,2,128]{4,3,2,1,0:T(2,128)S(1)}, f32[2,3,20,2,128]{4,3,2,1,0:T(2,128)S(1)}, u32[]{:S(2)}, u32[]{:S(2)}) collective-permute-start(f32[2,3,20,2,128]{4,3,2,1,0:T(2,128)S(1)} %get-tuple-element.153), channel_id=1, source_target_pairs={{1,0},{2,1},{3,2},{5,4},{6,5},{7,6},{9,8},{10,9},{11,10},{13,12},{... | collective-permute-start | bytes 368648 | tf_op jit(solution)/shard_map/ppermute | solution.py:24
  139.6 6.3 %collective-permute-start.16 = (f32[2,3,2,8,128]{4,3,2,1,0:T(8,128)S(1)}, f32[2,3,2,8,128]{4,3,2,1,0:T(8,128)S(1)}, u32[]{:S(2)}, u32[]{:S(2)}) collective-permute-start(f32[2,3,2,8,128]{4,3,2,1,0:T(8,128)S(1)} %get-tuple-element.223), channel_id=1, source_target_pairs={{4,0},{5,1},{6,2},{7,3},{12,8},{13,9},{14,10},{15,11},{20,16},{21,... | collective-permute-start | bytes 147464 | tf_op jit(solution)/shard_map/ppermute | solution.py:24
  146.0 6.8 %collective-permute-start.19 = (f32[2,3,20,2,128]{4,3,2,1,0:T(2,128)S(1)}, f32[2,3,20,2,128]{4,3,2,1,0:T(2,128)S(1)}, u32[]{:S(2)}, u32[]{:S(2)}) collective-permute-start(f32[2,3,20,2,128]{4,3,2,1,0:T(2,128)S(1)} %get-tuple-element.150), channel_id=1, source_target_pairs={{0,1},{1,2},{2,3},{4,5},{5,6},{6,7},{8,9},{9,10},{10,11},{12,13},{... | collective-permute-start | bytes 368648 | tf_op jit(solution)/shard_map/ppermute | solution.py:23
  147.3 7.0 %collective-permute-start.18 = (f32[2,3,20,2,128]{4,3,2,1,0:T(2,128)S(1)}, f32[2,3,20,2,128]{4,3,2,1,0:T(2,128)S(1)}, u32[]{:S(2)}, u32[]{:S(2)}) collective-permute-start(f32[2,3,20,2,128]{4,3,2,1,0:T(2,128)S(1)} %get-tuple-element.151), channel_id=1, source_target_pairs={{1,0},{2,1},{3,2},{5,4},{6,5},{7,6},{9,8},{10,9},{11,10},{13,12},{... | collective-permute-start | bytes 368648 | tf_op jit(solution)/shard_map/ppermute | solution.py:24
  182.9 6.3 %collective-permute-start.20 = (f32[2,3,2,8,128]{4,3,2,1,0:T(8,128)S(1)}, f32[2,3,2,8,128]{4,3,2,1,0:T(8,128)S(1)}, u32[]{:S(2)}, u32[]{:S(2)}) collective-permute-start(f32[2,3,2,8,128]{4,3,2,1,0:T(8,128)S(1)} %get-tuple-element.217), channel_id=1, source_target_pairs={{4,0},{5,1},{6,2},{7,3},{12,8},{13,9},{14,10},{15,11},{20,16},{21,... | collective-permute-start | bytes 147464 | tf_op jit(solution)/shard_map/ppermute | solution.py:24
  189.3 6.8 %collective-permute-start.23 = (f32[2,3,20,2,128]{4,3,2,1,0:T(2,128)S(1)}, f32[2,3,20,2,128]{4,3,2,1,0:T(2,128)S(1)}, u32[]{:S(2)}, u32[]{:S(2)}) collective-permute-start(f32[2,3,20,2,128]{4,3,2,1,0:T(2,128)S(1)} %get-tuple-element.148), channel_id=1, source_target_pairs={{0,1},{1,2},{2,3},{4,5},{5,6},{6,7},{8,9},{9,10},{10,11},{12,13},{... | collective-permute-start | bytes 368648 | tf_op jit(solution)/shard_map/ppermute | solution.py:23
  190.6 7.0 %collective-permute-start.22 = (f32[2,3,20,2,128]{4,3,2,1,0:T(2,128)S(1)}, f32[2,3,20,2,128]{4,3,2,1,0:T(2,128)S(1)}, u32[]{:S(2)}, u32[]{:S(2)}) collective-permute-start(f32[2,3,20,2,128]{4,3,2,1,0:T(2,128)S(1)} %get-tuple-element.149), channel_id=1, source_target_pairs={{1,0},{2,1},{3,2},{5,4},{6,5},{7,6},{9,8},{10,9},{11,10},{13,12},{... | collective-permute-start | bytes 368648 | tf_op jit(solution)/shard_map/ppermute | solution.py:24
  222.2 6.3 %collective-permute-start.24 = (f32[2,3,2,8,128]{4,3,2,1,0:T(8,128)S(1)}, f32[2,3,2,8,128]{4,3,2,1,0:T(8,128)S(1)}, u32[]{:S(2)}, u32[]{:S(2)}) collective-permute-start(f32[2,3,2,8,128]{4,3,2,1,0:T(8,128)S(1)} %get-tuple-element.213), channel_id=1, source_target_pairs={{4,0},{5,1},{6,2},{7,3},{12,8},{13,9},{14,10},{15,11},{20,16},{21,... | collective-permute-start | bytes 147464 | tf_op jit(solution)/shard_map/ppermute | solution.py:24
  228.6 6.8 %collective-permute-start.27 = (f32[2,3,20,2,128]{4,3,2,1,0:T(2,128)S(1)}, f32[2,3,20,2,128]{4,3,2,1,0:T(2,128)S(1)}, u32[]{:S(2)}, u32[]{:S(2)}) collective-permute-start(f32[2,3,20,2,128]{4,3,2,1,0:T(2,128)S(1)} %get-tuple-element.146), channel_id=1, source_target_pairs={{0,1},{1,2},{2,3},{4,5},{5,6},{6,7},{8,9},{9,10},{10,11},{12,13},{... | collective-permute-start | bytes 368648 | tf_op jit(solution)/shard_map/ppermute | solution.py:23
  229.9 7.0 %collective-permute-start.26 = (f32[2,3,20,2,128]{4,3,2,1,0:T(2,128)S(1)}, f32[2,3,20,2,128]{4,3,2,1,0:T(2,128)S(1)}, u32[]{:S(2)}, u32[]{:S(2)}) collective-permute-start(f32[2,3,20,2,128]{4,3,2,1,0:T(2,128)S(1)} %get-tuple-element.147), channel_id=1, source_target_pairs={{1,0},{2,1},{3,2},{5,4},{6,5},{7,6},{9,8},{10,9},{11,10},{13,12},{... | collective-permute-start | bytes 368648 | tf_op jit(solution)/shard_map/ppermute | solution.py:24
  273.1 6.8 %collective-permute-start.31 = (f32[2,3,20,2,128]{4,3,2,1,0:T(2,128)S(1)}, f32[2,3,20,2,128]{4,3,2,1,0:T(2,128)S(1)}, u32[]{:S(2)}, u32[]{:S(2)}) collective-permute-start(f32[2,3,20,2,128]{4,3,2,1,0:T(2,128)S(1)} %get-tuple-element.144), channel_id=1, source_target_pairs={{0,1},{1,2},{2,3},{4,5},{5,6},{6,7},{8,9},{9,10},{10,11},{12,13},{... | collective-permute-start | bytes 368648 | tf_op jit(solution)/shard_map/ppermute | solution.py:23
  274.4 7.0 %collective-permute-start.30 = (f32[2,3,20,2,128]{4,3,2,1,0:T(2,128)S(1)}, f32[2,3,20,2,128]{4,3,2,1,0:T(2,128)S(1)}, u32[]{:S(2)}, u32[]{:S(2)}) collective-permute-start(f32[2,3,20,2,128]{4,3,2,1,0:T(2,128)S(1)} %get-tuple-element.145), channel_id=1, source_target_pairs={{1,0},{2,1},{3,2},{5,4},{6,5},{7,6},{9,8},{10,9},{11,10},{13,12},{... | collective-permute-start | bytes 368648 | tf_op jit(solution)/shard_map/ppermute | solution.py:24
  315.3 6.8 %collective-permute-start.35 = (f32[2,3,20,2,128]{4,3,2,1,0:T(2,128)S(1)}, f32[2,3,20,2,128]{4,3,2,1,0:T(2,128)S(1)}, u32[]{:S(2)}, u32[]{:S(2)}) collective-permute-start(f32[2,3,20,2,128]{4,3,2,1,0:T(2,128)S(1)} %get-tuple-element.142), channel_id=1, source_target_pairs={{0,1},{1,2},{2,3},{4,5},{5,6},{6,7},{8,9},{9,10},{10,11},{12,13},{... | collective-permute-start | bytes 368648 | tf_op jit(solution)/shard_map/ppermute | solution.py:23
  316.6 7.0 %collective-permute-start.34 = (f32[2,3,20,2,128]{4,3,2,1,0:T(2,128)S(1)}, f32[2,3,20,2,128]{4,3,2,1,0:T(2,128)S(1)}, u32[]{:S(2)}, u32[]{:S(2)}) collective-permute-start(f32[2,3,20,2,128]{4,3,2,1,0:T(2,128)S(1)} %get-tuple-element.143), channel_id=1, source_target_pairs={{1,0},{2,1},{3,2},{5,4},{6,5},{7,6},{9,8},{10,9},{11,10},{13,12},{... | collective-permute-start | bytes 368648 | tf_op jit(solution)/shard_map/ppermute | solution.py:24
  (50 other events, 313.5 us)
where the time goes:
time: 356 us; the launch traced here: 351 us
  blocking collectives  159 us (45%)
  starting transfers between devices  106 us (30%)
  other arithmetic  41.9 us (12%)
  waiting for transfers between devices  35.5 us (10%)
  local copies, waits for them, and re-layouts  6.87 us (2%)
    ppermute x18, starting transfers between devices, with_halo(): after = lax.ppermute(leading, axis, down)  82.5 us
    psum x4, blocking collectives, shards(): lax.psum((cross_local[0], cross_local[1], norm_local, shadow_half[0], sha...  79.7 us
    psum x3, blocking collectives, shards(): lax.psum(braket(shadow, image), ('gx', 'gyz'))  59.1 us
    ppermute x18, waiting for transfers between devices, with_halo(): after = lax.ppermute(leading, axis, down)  26.8 us
    ppermute x18, starting transfers between devices, with_halo(): before = lax.ppermute(last, axis, up)  23.2 us
    psum x1, blocking collectives, shards(): rho_now = lax.psum(braket(shadow, residual), ('gx', 'gyz'))  20 us
    sub x11, other arithmetic, scale_complex(): real_coef * vector[0] - imag_coef * vector[1]  11.1 us
    concatenate x25, other arithmetic, with_halo(): array = jnp.concatenate([before, array, after], axis=dim)  10.8 us
  transfers between devices with their start and end apart: 36, of which 36 were waited for; matrix products, arithmetic and copies ran while one was open for 0% of the time, Pallas kernels for 0%

commit v1 on v0

--- a/solution.py
+++ b/solution.py
@@ -1,6 +1,10 @@
+import functools
+
 import jax
 import jax.numpy as jnp
 from jax import lax
+from jax.experimental import pallas as pl
+from jax.experimental.pallas import tpu as pltpu
 from jax.sharding import PartitionSpec as P
 
 ITERS = 4
@@ -152,9 +156,397 @@
     return (evolved, residual)
 
 
+LEAD = 8
+FIELD_BUDGET = 1 << 20
+NEAR = -0.5 / SPACING**2 * COEFF_NEAR * HALF_STEP
+FAR = -0.5 / SPACING**2 * COEFF_FAR * HALF_STEP
+
+
+def owner_of(orb, j, size_x, size_y):
+    odd = orb % 2
+    turn = j // size_x
+    return j % size_x, (size_y + size_y // 2 - 1 + odd + turn * (1 - 2 * odd)) % size_y
+
+
+def solve_kernel(
+    sizes,
+    orb_ref,
+    pot_ref,
+    evolved_ref,
+    residual_ref,
+    field,
+    hat_a,
+    hat_b,
+    shadow,
+    resid,
+    direction,
+    image,
+    second,
+    pot,
+    quot,
+    quot_d,
+    send_orb,
+    recv_orb,
+    send_pot,
+    recv_pot,
+    send_out,
+    recv_out,
+    local_sem,
+):
+    size_x, size_y = sizes
+    count, bx, by, nz = orb_ref.shape[1:]
+    nx, ny = (size_x * bx, size_y * by)
+    orb, gx, gy = (lax.axis_index("orb"), lax.axis_index("gx"), lax.axis_index("gyz"))
+    me = gx * size_y + gy
+    devices = size_x * size_y
+    owners = []
+    for j in range(count):
+        ox, oy = owner_of(orb, j, size_x, size_y)
+        owners.append((ox, oy, jnp.logical_and(ox == gx, oy == gy)))
+    mine = owners[0][2]
+    for j in range(1, count):
+        mine = jnp.logical_or(mine, owners[j][2])
+
+    barrier = pltpu.get_barrier_semaphore()
+    for dev in range(devices):
+        @pl.when(me != dev)
+        def _():
+            pl.semaphore_signal(
+                barrier,
+                inc=1,
+                device_id={"gx": dev // size_y, "gyz": dev % size_y},
+                device_id_type=pl.DeviceIdType.MESH,
+            )
+
+    @pl.when(mine)
+    def _():
+        for ref in (field, hat_a, hat_b):
+            edge = jnp.zeros((2, 2, ny + 2 * LEAD, nz), jnp.float32)
+            ref[:, 0:2] = edge
+            ref[:, nx + 2 : nx + 4] = edge
+
+            def clear(x, carry):
+                side = jnp.zeros((2, LEAD, nz), jnp.float32)
+                ref[:, x + 2, 0:LEAD] = side
+                ref[:, x + 2, LEAD + ny : 2 * LEAD + ny] = side
+                return carry
+
+            lax.fori_loop(0, nx, clear, 0)
+
+    pl.semaphore_wait(barrier, devices - 1)
+
+    def spot(ref, x_block, y_block):
+        return ref.at[:, pl.ds(2 + x_block * bx, bx), pl.ds(LEAD + y_block * by, by), :]
+
+    def pot_spot(ref, x_block, y_block):
+        return ref.at[pl.ds(x_block * bx, bx), pl.ds(y_block * by, by), :]
+
+    def inner_spot(ref, x_block, y_block):
+        return ref.at[:, pl.ds(x_block * bx, bx), pl.ds(y_block * by, by), :]
+
+    def remote(src, dst, send, recv, x, y):
+        return pltpu.make_async_remote_copy(
+            src_ref=src,
+            dst_ref=dst,
+            send_sem=send,
+            recv_sem=recv,
+            device_id={"gx": x, "gyz": y},
+            device_id_type=pl.DeviceIdType.MESH,
+        )
+
+    def gather_copies(j):
+        ox, oy, own = owners[j]
+        return (
+            remote(orb_ref.at[:, j], spot(field, gx, gy), send_orb.at[j], recv_orb.at[me], ox, oy),
+            remote(pot_ref, pot_spot(pot, gx, gy), send_pot.at[j], recv_pot.at[me], ox, oy),
+        )
+
+    def local_copies(j):
+        return (
+            pltpu.make_async_copy(orb_ref.at[:, j], spot(field, gx, gy), local_sem.at[0]),
+            pltpu.make_async_copy(pot_ref, pot_spot(pot, gx, gy), local_sem.at[1]),
+        )
+
+    for j in range(count):
+        own = owners[j][2]
+
+        @pl.when(jnp.logical_not(own))
+        def _():
+            for copy in gather_copies(j):
+                copy.start()
+
+        @pl.when(own)
+        def _():
+            for copy in local_copies(j):
+                copy.start()
+
+    lane = lax.broadcasted_iota(jnp.int32, (ny, nz), 1)
+
+    def neighbours(ref, part, x):
+        def at(dx, dy):
+            return ref[part, x + 2 + dx, LEAD + dy : LEAD + dy + ny, :]
+
+        center = at(0, 0)
+        near = (at(1, 0) + at(-1, 0)) + (at(0, 1) + at(0, -1))
+        far = (at(2, 0) + at(-2, 0)) + (at(0, 2) + at(0, -2))
+        near = near + (
+            jnp.where(lane < 1, 0.0, pltpu.roll(center, 1, 1))
+            + jnp.where(lane >= nz - 1, 0.0, pltpu.roll(center, nz - 1, 1))
+        )
+        far = far + (
+            jnp.where(lane < 2, 0.0, pltpu.roll(center, 2, 1))
+            + jnp.where(lane >= nz - 2, 0.0, pltpu.roll(center, nz - 2, 1))
+        )
+        return NEAR * near + FAR * far, center
+
+    def fold(value):
+        return jnp.sum(value.reshape(ny // 8, 8, nz), axis=0)
+
+    def total(value):
+        return jnp.sum(value, keepdims=True)
+
+    zero = jnp.zeros((8, nz), jnp.float32)
+    rows = slice(LEAD, LEAD + ny)
+
+    def set_hat(hat, x, re, im):
+        q, qd = (quot[x], quot_d[x])
+        hat[0, x + 2, rows, :] = q * re + qd * im
+        hat[1, x + 2, rows, :] = q * im - qd * re
+
+    def start_plane(x, rho):
+        d = HALF_STEP * (-1.5 * COEFF_SELF / SPACING**2 + pot[x])
+        q = 1.0 / (1.0 + d * d)
+        quot[x] = q
+        quot_d[x] = q * d
+        off_re, re = neighbours(field, 0, x)
+        off_im, im = neighbours(field, 1, x)
+        r_re = 2.0 * (off_im + d * im)
+        r_im = -2.0 * (off_re + d * re)
+        for ref in (shadow, resid, direction):
+            ref[0, x] = r_re
+            ref[1, x] = r_im
+        set_hat(hat_a, x, r_re, r_im)
+        return rho + fold(r_re * r_re + r_im * r_im)
+
+    def image_plane(x, sums):
+        off_re, _ = neighbours(hat_a, 0, x)
+        off_im, _ = neighbours(hat_a, 1, x)
+        i_re = direction[0, x] - off_im
+        i_im = direction[1, x] + off_re
+        image[0, x] = i_re
+        image[1, x] = i_im
+        s_re, s_im = (shadow[0, x], shadow[1, x])
+        return (
+            sums[0] + fold(s_re * i_re + s_im * i_im),
+            sums[1] + fold(s_re * i_im - s_im * i_re),
+        )
+
+    def half_plane(alpha, x, sums):
+        i_re, i_im = (image[0, x], image[1, x])
+        h_re = resid[0, x] - (alpha[0] * i_re - alpha[1] * i_im)
+        h_im = resid[1, x] - (alpha[0] * i_im + alpha[1] * i_re)
+        resid[0, x] = h_re
+        resid[1, x] = h_im
+        set_hat(hat_b, x, h_re, h_im)
+        s_re, s_im = (shadow[0, x], shadow[1, x])
+        return (
+            sums[0] + fold(s_re * h_re + s_im * h_im),
+            sums[1] + fold(s_re * h_im - s_im * h_re),
+        )
+
+    def second_plane(x, sums):
+        off_re, _ = neighbours(hat_b, 0, x)
+        off_im, _ = neighbours(hat_b, 1, x)
+        h_re, h_im = (resid[0, x], resid[1, x])
+        t_re = h_re - off_im
+        t_im = h_im + off_re
+        second[0, x] = t_re
+        second[1, x] = t_im
+        s_re, s_im = (shadow[0, x], shadow[1, x])
+        return (
+            sums[0] + fold(t_re * h_re + t_im * h_im),
+            sums[1] + fold(t_re * h_im - t_im * h_re),
+            sums[2] + fold(t_re * t_re + t_im * t_im),
+            sums[3] + fold(s_re * t_re + s_im * t_im),
+            sums[4] + fold(s_re * t_im - s_im * t_re),
+        )
+
+    def update_plane(alpha, omega, x):
+        a_re, a_im = (hat_a[0, x + 2, rows, :], hat_a[1, x + 2, rows, :])
+        b_re, b_im = (hat_b[0, x + 2, rows, :], hat_b[1, x + 2, rows, :])
+        t_re, t_im = (second[0, x], second[1, x])
+        field[0, x + 2, rows, :] = (
+            field[0, x + 2, rows, :]
+            + (alpha[0] * a_re - alpha[1] * a_im)
+            + (omega[0] * b_re - omega[1] * b_im)
+        )
+        field[1, x + 2, rows, :] = (
+            field[1, x + 2, rows, :]
+            + (alpha[0] * a_im + alpha[1] * a_re)
+            + (omega[0] * b_im + omega[1] * b_re)
+        )
+        r_re = resid[0, x] - (omega[0] * t_re - omega[1] * t_im)
+        r_im = resid[1, x] - (omega[0] * t_im + omega[1] * t_re)
+        resid[0, x] = r_re
+        resid[1, x] = r_im
+        return r_re, r_im
+
+    def next_plane(alpha, omega, beta, x, carry):
+        r_re, r_im = update_plane(alpha, omega, x)
+        i_re, i_im = (image[0, x], image[1, x])
+        u_re = direction[0, x] - (omega[0] * i_re - omega[1] * i_im)
+        u_im = direction[1, x] - (omega[0] * i_im + omega[1] * i_re)
+        d_re = r_re + (beta[0] * u_re - beta[1] * u_im)
+        d_im = r_im + (beta[0] * u_im + beta[1] * u_re)
+        direction[0, x] = d_re
+        direction[1, x] = d_im
+        set_hat(hat_a, x, d_re, d_im)
+        return carry
+
+    def out_copies(j, x, y):
+        slot = x * size_y + y
+        return (
+            remote(
+                spot(field, x, y), evolved_ref.at[:, j], send_out.at[0, slot], recv_out.at[0, j], x, y
+            ),
+            remote(
+                inner_spot(resid, x, y),
+                residual_ref.at[:, j],
+                send_out.at[1, slot],
+                recv_out.at[1, j],
+                x,
+                y,
+            ),
+        )
+
+    def out_local(j):
+        return (
+            pltpu.make_async_copy(spot(field, gx, gy), evolved_ref.at[:, j], local_sem.at[0]),
+            pltpu.make_async_copy(inner_spot(resid, gx, gy), residual_ref.at[:, j], local_sem.at[1]),
+        )
+
+    def each_out(x, act):
+        for j in range(count):
+            for y in range(size_y):
+                other = jnp.logical_or(gx != x, gy != y)
+
+                @pl.when(jnp.logical_and(owners[j][2], other))
+                def _():
+                    for copy in out_copies(j, x, y):
+                        act(copy)
+
+                @pl.when(jnp.logical_and(owners[j][2], jnp.logical_not(other)))
+                def _():
+                    for copy in out_local(j):
+                        if act is begin:
+                            copy.start()
+                        else:
+                            copy.wait()
+
+    def begin(copy):
+        copy.start()
+
+    def finish(copy):
+        copy.wait_send()
+
+    @pl.when(mine)
+    def _():
+        for dev in range(devices):
+            x, y = (dev // size_y, dev % size_y)
+
+            @pl.when(me != dev)
+            def _():
+                remote(
+                    orb_ref.at[:, 0], spot(field, x, y), send_orb.at[0], recv_orb.at[dev], x, y
+                ).wait_recv()
+                remote(
+                    pot_ref, pot_spot(pot, x, y), send_pot.at[0], recv_pot.at[dev], x, y
+                ).wait_recv()
+
+        for copy in local_copies(0):
+            copy.wait()
+
+        rho_sum = lax.fori_loop(0, nx, start_plane, zero)
+        rho = (total(rho_sum), jnp.zeros((1, 1), jnp.float32))
+        for iteration in range(ITERS):
+            sums = lax.fori_loop(0, nx, image_plane, (zero, zero))
+            alpha = divide_complex(rho, (total(sums[0]), total(sums[1])))
+            held = lax.fori_loop(0, nx, functools.partial(half_plane, alpha), (zero, zero))
+            sums = lax.fori_loop(0, nx, second_plane, (zero,) * 5)
+            norm = total(sums[2])
+            omega = (total(sums[0]) / norm, total(sums[1]) / norm)
+            if iteration + 1 < ITERS:
+                along = times_complex(omega, (total(sums[3]), total(sums[4])))
+                rho_next = (total(held[0]) - along[0], total(held[1]) - along[1])
+                beta = times_complex(divide_complex(rho_next, rho), divide_complex(alpha, omega))
+                rho = rho_next
+                lax.fori_loop(0, nx, functools.partial(next_plane, alpha, omega, beta), 0)
+
+        def last_plane(x, carry):
+            update_plane(alpha, omega, x)
+            return carry
+
+        for x in range(size_x):
+            lax.fori_loop(x * bx, (x + 1) * bx, last_plane, 0)
+            each_out(x, begin)
+        for x in range(size_x):
+            each_out(x, finish)
+
+    for j in range(count):
+        @pl.when(jnp.logical_not(owners[j][2]))
+        def _():
+            for copy in gather_copies(j):
+                copy.wait_send()
+            for copy in out_copies(j, 0, 0):
+                copy.wait_recv()
+
+
+def gathered(sizes, orbitals, potential):
+    size_x, size_y = sizes
+    _, count, bx, by, nz = orbitals.shape
+    nx, ny = (size_x * bx, size_y * by)
+    padded = pltpu.VMEM((2, nx + 4, ny + 2 * LEAD, nz), jnp.float32)
+    plain = pltpu.VMEM((2, nx, ny, nz), jnp.float32)
+    scalar = pltpu.VMEM((nx, ny, nz), jnp.float32)
+    dma = pltpu.SemaphoreType.DMA
+    devices = size_x * size_y
+    shape = jax.ShapeDtypeStruct(orbitals.shape, jnp.float32)
+    return pl.pallas_call(
+        functools.partial(solve_kernel, sizes),
+        out_shape=(shape, shape),
+        in_specs=[pl.BlockSpec(memory_space=pltpu.VMEM)] * 2,
+        out_specs=(pl.BlockSpec(memory_space=pltpu.VMEM),) * 2,
+        scratch_shapes=[padded] * 3
+        + [plain] * 5
+        + [scalar] * 3
+        + [
+            dma((count,)),
+            dma((devices,)),
+            dma((count,)),
+            dma((devices,)),
+            dma((2, devices)),
+            dma((2, count)),
+            dma((2,)),
+        ],
+        compiler_params=pltpu.CompilerParams(
+            collective_id=0, has_side_effects=True, vmem_limit_bytes=48 * 1024 * 1024
+        ),
+    )(orbitals, potential)
+
+
+def step(sizes, orbitals, potential):
+    _, count, bx, by, nz = orbitals.shape
+    devices = sizes[0] * sizes[1]
+    fits = 8 * devices * bx * by * nz <= FIELD_BUDGET
+    if fits and count <= devices and by % 8 == 0 and nz % 128 == 0:
+        return gathered(sizes, orbitals, potential)
+    return shards(orbitals, potential)
+
+
 def solution(mesh):
+    sizes = (mesh.shape["gx"], mesh.shape["gyz"])
     return jax.shard_map(
-        shards,
+        functools.partial(step, sizes),
         mesh=mesh,
         in_specs=(P(None, "orb", "gx", "gyz", None), P("gx", "gyz", None)),
         out_specs=(P(None, "orb", "gx", "gyz", None), P(None, "orb", "gx", "gyz", None)),

time: 356 us -> 89.4 us (0.25); the launches traced: 351 us -> 88.1 us
  blocking collectives: 159 us -> 0 us
  starting transfers between devices: 106 us -> 0 us
  Pallas kernels: 0 us -> 84.1 us
  other arithmetic: 41.9 us -> 0 us
  waiting for transfers between devices: 35.5 us -> 0 us
    psum x8 -> x0, blocking collectives: 159 us -> none  [the longest x4 79.7 us: shards(): lax.psum((cross_local[0], cross_local[1], norm_local, shadow_half[0], sha...]
    ppermute x36 -> x0, starting transfers between devices: 106 us -> none  [the longest x18 82.5 us: with_halo(): after = lax.ppermute(leading, axis, down)]
    pallas_call x0 -> x1, Pallas kernels: none -> 84.1 us  [gathered(): pl.pallas_call(functools.partial(solve_kernel, sizes), out_shape=(shape,...]
    ppermute x36 -> x0, waiting for transfers between devices: 35.5 us -> none  [the longest x18 26.8 us: with_halo(): after = lax.ppermute(leading, axis, down)]
    sub x29 -> x0, other arithmetic: 18.4 us -> none  [the longest x11 11.1 us: scale_complex(): real_coef * vector[0] - imag_coef * vector[1]]
    concatenate x25 -> x0, other arithmetic: 10.8 us -> none  [with_halo(): array = jnp.concatenate([before, array, after], axis=dim)]
    add x22 -> x0, other arithmetic: 7.59 us -> none  [the longest x9 5.71 us: laplace_apply(): return -0.5 / SPACING ** 2 * summed + potential * center]
    reduce_sum x12 -> x0, other arithmetic: 4.49 us -> none  [the longest x3 2.25 us: braket(): imag_part = jnp.sum(left[0] * right[1] - left[1] * right[0], axis=(1, 2, 3))]
  transfers between devices with their start and end apart: 36 -> 0, of which waited for: 36 -> 0; matrix products, arithmetic and copies ran while one was open for 0% -> 0% of each run, Pallas kernels for 0% -> 0%
where the time goes in v1:
time: 89.4 us; the launch traced here: 88.1 us
  Pallas kernels  84.1 us (94%)
  local copies, waits for them, and re-layouts  3.32 us (4%)
    pallas_call x1, Pallas kernels, gathered(): pl.pallas_call(functools.partial(solve_kernel, sizes), out_shape=(shape,...  84.1 us
    unnamed x6, local copies, waits for them, and re-layouts  3.32 us

profile of v1, /device:TPU:28, one launch (start us, length us, event | category | flops | bytes accessed | tf_op | source)
XLA Modules:
  0.0 88.1 jit_solution(2927431482585417420)
XLA Ops:
  0.6 0.0 copy-start
  0.6 1.0 %copy-done = f32[2,3,16,8,128]{4,3,2,1,0:T(8,128)S(1)} copy-done((f32[2,3,16,8,128]{4,3,2,1,0:T(8,128)S(1)}, f32[2,3,16,8,128]{4,3,2,1,0:T(8,128)}, u32[]{:S(2)}) %copy-start) | copy-done | bytes 393240
  1.6 0.0 copy-start.1
  1.6 0.8 copy-done.1
  2.5 84.1 %shard_map.41 = (f32[2,3,16,8,128]{4,3,2,1,0:T(8,128)S(1)}, f32[2,3,16,8,128]{4,3,2,1,0:T(8,128)S(1)}) custom-call(f32[2,3,16,8,128]{4,3,2,1,0:T(8,128)S(1)} %copy-done, f32[16,8,128]{2,1,0:T(8,128)S(1)} %copy-done.1), custom_call_target="tpu_custom_call" | custom-call | tf_op jit(solution)/shard_map/pallas_call | solution.py:514
  86.6 0.7 copy.6
  87.3 0.7 copy.7
Async XLA Ops:
  0.6 1.0 %copy-start = (f32[2,3,16,8,128]{4,3,2,1,0:T(8,128)S(1)}, f32[2,3,16,8,128]{4,3,2,1,0:T(8,128)}, u32[]{:S(2)}) copy-start(f32[2,3,16,8,128]{4,3,2,1,0:T(8,128)} %orb_ref.1) | copy-start | bytes 1179652
  1.6 0.8 copy-start.1

commit v2 on v1

--- a/solution.py
+++ b/solution.py
@@ -156,16 +156,29 @@
     return (evolved, residual)
 
 
+UNROLL = 8
 LEAD = 8
 FIELD_BUDGET = 1 << 20
 NEAR = -0.5 / SPACING**2 * COEFF_NEAR * HALF_STEP
 FAR = -0.5 / SPACING**2 * COEFF_FAR * HALF_STEP
 
 
-def owner_of(orb, j, size_x, size_y):
-    odd = orb % 2
-    turn = j // size_x
-    return j % size_x, (size_y + size_y // 2 - 1 + odd + turn * (1 - 2 * odd)) % size_y
+def owner_of(odd, j, size_x, size_y):
+    middle = size_y // 2
+    if odd:
+        return (1 + j // size_x) % size_x, (middle + j) % size_y
+    return j % size_x, (size_y + middle - 1 + j // size_x) % size_y
+
+
+def sweep(start, stop, plane, carry):
+    width = UNROLL if (stop - start) % UNROLL == 0 else 1
+
+    def group(i, carry):
+        for k in range(width):
+            carry = plane(start + i * width + k, carry)
+        return carry
+
+    return lax.fori_loop(0, (stop - start) // width, group, carry)
 
 
 def solve_kernel(
@@ -201,7 +214,9 @@
     devices = size_x * size_y
     owners = []
     for j in range(count):
-        ox, oy = owner_of(orb, j, size_x, size_y)
+        even, odd = (owner_of(parity, j, size_x, size_y) for parity in (0, 1))
+        ox = jnp.where(orb % 2 == 1, odd[0], even[0])
+        oy = jnp.where(orb % 2 == 1, odd[1], even[1])
         owners.append((ox, oy, jnp.logical_and(ox == gx, oy == gy)))
     mine = owners[0][2]
     for j in range(1, count):
@@ -466,13 +481,13 @@
         for copy in local_copies(0):
             copy.wait()
 
-        rho_sum = lax.fori_loop(0, nx, start_plane, zero)
+        rho_sum = sweep(0, nx, start_plane, zero)
         rho = (total(rho_sum), jnp.zeros((1, 1), jnp.float32))
         for iteration in range(ITERS):
-            sums = lax.fori_loop(0, nx, image_plane, (zero, zero))
+            sums = sweep(0, nx, image_plane, (zero, zero))
             alpha = divide_complex(rho, (total(sums[0]), total(sums[1])))
-            held = lax.fori_loop(0, nx, functools.partial(half_plane, alpha), (zero, zero))
-            sums = lax.fori_loop(0, nx, second_plane, (zero,) * 5)
+            held = sweep(0, nx, functools.partial(half_plane, alpha), (zero, zero))
+            sums = sweep(0, nx, second_plane, (zero,) * 5)
             norm = total(sums[2])
             omega = (total(sums[0]) / norm, total(sums[1]) / norm)
             if iteration + 1 < ITERS:
@@ -480,14 +495,14 @@
                 rho_next = (total(held[0]) - along[0], total(held[1]) - along[1])
                 beta = times_complex(divide_complex(rho_next, rho), divide_complex(alpha, omega))
                 rho = rho_next
-                lax.fori_loop(0, nx, functools.partial(next_plane, alpha, omega, beta), 0)
+                sweep(0, nx, functools.partial(next_plane, alpha, omega, beta), 0)
 
         def last_plane(x, carry):
             update_plane(alpha, omega, x)
             return carry
 
         for x in range(size_x):
-            lax.fori_loop(x * bx, (x + 1) * bx, last_plane, 0)
+            sweep(x * bx, (x + 1) * bx, last_plane, 0)
             each_out(x, begin)
         for x in range(size_x):
             each_out(x, finish)
@@ -538,7 +553,10 @@
     _, count, bx, by, nz = orbitals.shape
     devices = sizes[0] * sizes[1]
     fits = 8 * devices * bx * by * nz <= FIELD_BUDGET
-    if fits and count <= devices and by % 8 == 0 and nz % 128 == 0:
+    distinct = all(
+        len({owner_of(parity, j, *sizes) for j in range(count)}) == count for parity in (0, 1)
+    )
+    if fits and distinct and by % 8 == 0 and nz % 128 == 0:
         return gathered(sizes, orbitals, potential)
     return shards(orbitals, potential)
 

time: 89.4 us -> 62 us (0.69); the launches traced: 88.1 us -> 61.8 us
  Pallas kernels: 84.1 us -> 57.8 us
    pallas_call x1, Pallas kernels: 84.1 us -> 57.8 us  [gathered(): pl.pallas_call(functools.partial(solve_kernel, sizes), out_shape=(shape,...]
where the time goes in v2:
time: 62 us; the launch traced here: 61.8 us
  Pallas kernels  57.8 us (93%)
  local copies, waits for them, and re-layouts  3.32 us (5%)
  between operations  0.65 us (1%)
    pallas_call x1, Pallas kernels, gathered(): pl.pallas_call(functools.partial(solve_kernel, sizes), out_shape=(shape,...  57.8 us
    unnamed x6, local copies, waits for them, and re-layouts  3.32 us

profile of v2, /device:TPU:28, one launch (start us, length us, event | category | flops | bytes accessed | tf_op | source)
XLA Modules:
  0.0 61.8 jit_solution(5885481776556637258)
XLA Ops:
  0.6 0.0 copy-start
  0.6 1.0 %copy-done = f32[2,3,16,8,128]{4,3,2,1,0:T(8,128)S(1)} copy-done((f32[2,3,16,8,128]{4,3,2,1,0:T(8,128)S(1)}, f32[2,3,16,8,128]{4,3,2,1,0:T(8,128)}, u32[]{:S(2)}) %copy-start) | copy-done | bytes 393240
  1.6 0.0 copy-start.1
  1.6 0.8 %copy-done.1 = f32[16,8,128]{2,1,0:T(8,128)S(1)} copy-done((f32[16,8,128]{2,1,0:T(8,128)S(1)}, f32[16,8,128]{2,1,0:T(8,128)}, u32[]{:S(2)}) %copy-start.1) | copy-done | bytes 65560
  2.5 57.8 %shard_map.41 = (f32[2,3,16,8,128]{4,3,2,1,0:T(8,128)S(1)}, f32[2,3,16,8,128]{4,3,2,1,0:T(8,128)S(1)}) custom-call(f32[2,3,16,8,128]{4,3,2,1,0:T(8,128)S(1)} %copy-done, f32[16,8,128]{2,1,0:T(8,128)S(1)} %copy-done.1), custom_call_target="tpu_custom_call" | custom-call | tf_op jit(solution)/shard_map/pallas_call | solution.py:529
  60.3 0.7 %copy.6 = f32[2,3,16,8,128]{4,3,2,1,0:T(8,128)} copy(f32[2,3,16,8,128]{4,3,2,1,0:T(8,128)S(1)} %get-tuple-element.4) | data formatting | bytes 786432
  61.0 0.7 %copy.7 = f32[2,3,16,8,128]{4,3,2,1,0:T(8,128)} copy(f32[2,3,16,8,128]{4,3,2,1,0:T(8,128)S(1)} %get-tuple-element.5) | data formatting | bytes 786432
Async XLA Ops:
  0.6 1.0 %copy-start = (f32[2,3,16,8,128]{4,3,2,1,0:T(8,128)S(1)}, f32[2,3,16,8,128]{4,3,2,1,0:T(8,128)}, u32[]{:S(2)}) copy-start(f32[2,3,16,8,128]{4,3,2,1,0:T(8,128)} %orb_ref.1) | copy-start | bytes 1179652
  1.6 0.8 %copy-start.1 = (f32[16,8,128]{2,1,0:T(8,128)S(1)}, f32[16,8,128]{2,1,0:T(8,128)}, u32[]{:S(2)}) copy-start(f32[16,8,128]{2,1,0:T(8,128)} %pot_ref.1) | copy-start | bytes 196612
